TPU v7x, 32 devices: a whole 2x2x4 slice. The times are simulated.
32 devices in a mesh: dp: 8 (over z, x), mp: 4 (over y, core).
Axes of the slice: x: 2, y: 2, z: 4, core: 2. Of those that a mesh axis runs over, the one named last changes fastest.
Arguments:
- hidden_in: bfloat16 [8192, 2048], P('dp', 'mp'), may hold values from -6 to 6
- token_ids: int32 [8192], P('dp'), may hold values from 0 to 128001, as said below
- passage_counts: int32 [16], P('dp'), may hold values from 1 to 4, as said below
- positive_doc: int32 [1024], P('dp'), may hold values from 0 to 15
- queries: bfloat16 [1024, 2048], P('dp', 'mp'), may hold values from -6 to 6
- norm_gain: float32 [2048], replicated, may hold values from 0.5 to 1.5
- w_gate: bfloat16 [2048, 7168], P(None, 'mp'), may hold values from -0.125 to 0.125
- w_up: bfloat16 [2048, 7168], P(None, 'mp'), may hold values from -0.125 to 0.125
- w_down: bfloat16 [7168, 2048], P('mp'), may hold values from -0.0625 to 0.0625
Outputs:
- query_loss: float32 [1024], P('dp')
- hidden_grad: bfloat16 [8192, 2048], P('dp', 'mp')
Inputs may be any that keep to these rules, and one draw needn't show every extreme that they name: `passage_counts`: A document has 1 to 4 passages; every draw has a dp index whose documents all have 4. The live passages hold 40 passages in all. `token_ids`: 128001 marks padding; it stands only at the tail of a document's last live passage, and every live passage has a token that is not padding.
All inputs are finite; a program needn't handle non-finite values.
Results may differ from a plain program's by a relative error of at most 0.023.
Values may be sent and summed in bfloat16 or wider, within the bound.
A program may use at most 128 MiB of HBM per device.

v0:
```python
import functools

import jax
import jax.numpy as jnp
from jax import lax
from jax.experimental import pallas as pl
from jax.experimental.pallas import tpu as pltpu
from jax.sharding import PartitionSpec as P

L = 128

pad_token = 128001
score_scale = 20.0
loss_seed = 4096.0
norm_epsilon = 1e-05
unit_epsilon = 1e-06
lane = 128
chunk_pass = 2
MESH = pl.DeviceIdType.MESH
f32 = jnp.float32
bf16 = jnp.bfloat16


def dot_nn(left, right):
    return lax.dot_general(left, right, (((1,), (0,)), ((), ())), preferred_element_type=f32)


def dot_nt(left, right):
    return lax.dot_general(left, right, (((1,), (1,)), ((), ())), preferred_element_type=f32)


def tile_of(width):
    return 256 if width % 256 == 0 else lane


def kernel(
    dims,
    hidden, queries, w_gate, w_up, w_down, tokens, counts, positive, gain,
    loss_out, grad_out,
    x_buf, q_buf, wg, wu, wd, a_buf, b_buf, c_buf, normed, act, dgate, dup, rms,
    act_pool, row_pool, branch, everyone, term_send, term_recv, tok_grad, g_row, inner_x,
    mask_row, near_send, near_recv, far_send, far_recv, kept, staged,
    load_sem, out_sem, xn_s, xn_r, xf_s, xf_r, xr_s, xr_r, br_s, br_r, in_s, in_r,
    ev_s, ev_r, tm_s, tm_r, ns_s, ns_r, fs_s, fs_r,
):
    dp, mp, far, rows, width, model, hid, passes, most, chunks, crow = dims
    me = lax.axis_index("mp")
    dme = lax.axis_index("dp")
    chip, core = me // 2, me % 2
    partner = chip * 2 + (1 - core)

    def same(j):
        return ((chip + j + far) % far) * 2 + core

    def other(j):
        return ((chip + j + far) % far) * 2 + (1 - core)

    def chunk_rows(c):
        return pl.ds(pl.multiple_of(c * crow, crow), crow)

    def remote(src, dst, send, recv, d, m):
        return pltpu.make_async_remote_copy(
            src_ref=src, dst_ref=dst, send_sem=send, recv_sem=recv,
            device_id=(d, m), device_id_type=MESH,
        )

    load_x = pltpu.make_async_copy(hidden, x_buf.at[me], load_sem.at[0])
    load_g = pltpu.make_async_copy(w_gate, wg, load_sem.at[1])
    load_u = pltpu.make_async_copy(w_up, wu, load_sem.at[2])
    load_d = pltpu.make_async_copy(w_down, wd, load_sem.at[3])
    load_q = pltpu.make_async_copy(queries, q_buf.at[me], load_sem.at[4])

    barrier = pltpu.get_barrier_semaphore()
    for k in range(1, mp):
        pl.semaphore_signal(barrier, inc=1, device_id=(dme, (me + k) % mp), device_id_type=MESH)
    for k in range(1, dp):
        pl.semaphore_signal(barrier, inc=1, device_id=((dme + k) % dp, me), device_id_type=MESH)
    load_x.start()
    load_g.start()
    load_u.start()
    load_q.start()
    load_d.start()
    pl.semaphore_wait(barrier, mp - 1 + dp - 1)

    def piece(ref, c):
        return ref.at[chunk_rows(c)] if not isinstance(c, int) or c < chunks else ref

    def far_copy(j, c):
        if isinstance(c, int) and c == chunks:
            src, dst = queries, q_buf.at[me]
        else:
            src, dst = hidden.at[chunk_rows(c)], x_buf.at[me, chunk_rows(c)]
        return remote(src, dst, xf_s.at[j - 1, c], xf_r.at[j - 1, c], dme, same(j))

    def near_copy(c):
        if isinstance(c, int) and c == chunks:
            src, dst = queries, q_buf.at[me]
        else:
            src, dst = hidden.at[chunk_rows(c)], x_buf.at[me, chunk_rows(c)]
        return remote(src, dst, xn_s.at[c], xn_r.at[c], dme, partner)

    def relay_copy(j, c):
        if isinstance(c, int) and c == chunks:
            src = dst = q_buf.at[same(-j)]
        else:
            src = dst = x_buf.at[same(-j), chunk_rows(c)]
        return remote(src, dst, xr_s.at[j - 1, c], xr_r.at[j - 1, c], dme, partner)

    def relay(c):
        for j in range(1, far):
            far_copy(j, c).wait_recv()
            relay_copy(j, c).start()

    for c in range(chunks + 1):
        for j in range(1, far):
            far_copy(j, c).start()
        near_copy(c).start()

    pass_index = lax.broadcasted_iota(jnp.int32, (passes, L), 0)
    count = jnp.zeros((passes, L), jnp.int32)
    for d in range(passes // most):
        count = jnp.where(pass_index // most == d, counts[d], count)
    live = (pass_index % most < count).astype(f32)
    mask = jnp.where(tokens[...] != pad_token, live, 0.0)
    mask_row[...] = mask
    divisor = jnp.maximum(jnp.sum(mask, axis=1, keepdims=True), 1.0)
    act_pool[...] = jnp.zeros_like(act_pool)
    row_pool[...] = jnp.zeros_like(row_pool)
    pool_index = lax.broadcasted_iota(jnp.int32, (2 * passes, L), 0)

    tile = tile_of(hid)
    relay(0)
    load_x.wait()
    load_g.wait()
    load_u.wait()

    def forward(c, carry):
        at = chunk_rows(c)
        near_copy(c).wait_recv()
        for j in range(1, far):
            relay_copy(j, c).wait_recv()
        squares = jnp.zeros((crow, 1), f32)
        select = jnp.concatenate(
            [
                jnp.where(pool_index == c * chunk_pass + i, mask_row[pl.ds(c * chunk_pass + i, 1), :], 0.0)
                for i in range(chunk_pass)
            ],
            axis=1,
        ).astype(bf16)
        for m in range(mp):
            piece_x = x_buf[m, at, :].astype(f32)
            squares = squares + jnp.sum(piece_x * piece_x, axis=1, keepdims=True)
        scale = lax.rsqrt(squares / model + norm_epsilon)
        rms[at, :] = scale
        for m in range(mp):
            cols = slice(m * width, (m + 1) * width)
            raw_x = x_buf[m, at, :]
            normed[:, cols] = (raw_x.astype(f32) * scale * gain[:, cols]).astype(bf16)
            row_pool[:, cols] += dot_nn(select, raw_x)
        for t in range(hid // tile):
            cols = slice(t * tile, (t + 1) * tile)
            gate = dot_nn(normed[...], wg[:, cols])
            up = dot_nn(normed[...], wu[:, cols])
            sig = jax.nn.sigmoid(gate)
            b = gate * sig
            a = up * sig * (1.0 + gate * (1.0 - sig))
            hidden_act = (b * up).astype(bf16)
            a_buf[at, cols] = a.astype(bf16)
            b_buf[at, cols] = b.astype(bf16)
            c_buf[at, cols] = (a * gate + b * up).astype(bf16)
            act_pool[:, cols] += dot_nn(select, hidden_act)
            if t == max(hid // tile - 2, 0):
                @pl.when(c + 1 < chunks)
                def _():
                    relay(c + 1)
        return carry

    lax.fori_loop(0, chunks, forward, 0)
    relay(chunks)

    load_d.wait()
    pooled = act_pool[0:passes, :]
    high = pooled.astype(bf16).astype(f32)
    both = jnp.concatenate([high, pooled - high], axis=0).astype(bf16)
    for m in range(mp):
        cols = slice(m * width, (m + 1) * width)
        part = dot_nn(both, wd[:, cols])
        branch[me, :, cols] = (part[0:passes] + part[passes:]).astype(bf16)

    def branch_copy(k):
        return remote(
            branch.at[me], branch.at[me], br_s.at[k - 1], br_r.at[k - 1], dme, (me + k) % mp
        )

    for k in range(1, mp):
        branch_copy(k).start()

    load_q.wait()
    near_copy(chunks).wait_recv()
    for j in range(1, far):
        relay_copy(j, chunks).wait_recv()
    ones = jnp.ones((2 * passes, width), bf16)
    query_square = jnp.zeros((2 * passes, q_buf.shape[1]), f32)
    for m in range(mp):
        query = q_buf[m].astype(f32)
        square = query * query
        top = square.astype(bf16)
        rest = (square - top.astype(f32)).astype(bf16)
        query_square = query_square + dot_nt(ones, top) + dot_nt(ones, rest)
    query_scale = lax.rsqrt(query_square[0:1, :] + unit_epsilon)

    for k in range(1, mp):
        branch_copy(k).wait_recv()
    total = row_pool[0:passes, :]
    for m in range(mp):
        total = total + branch[m].astype(f32)
    everyone[dme, :, 0:model] = (total / divisor).astype(bf16)
    everyone[dme, :, model:] = live.astype(bf16)

    def every_copy(k):
        return remote(
            everyone.at[dme], everyone.at[dme], ev_s.at[k - 1], ev_r.at[k - 1], (dme + k) % dp, me
        )

    for k in range(1, dp):
        every_copy(k).start()
    for k in range(1, dp):
        every_copy(k).wait_recv()

    slabs = [everyone[d].astype(f32) for d in range(dp)]
    slab = jnp.concatenate(slabs, axis=0)
    vec = slab[:, 0:model]
    all_live = slab[:, model : model + 1]
    vec_half = vec.astype(bf16)
    pass_total = dp * passes
    raw = jnp.zeros((pass_total, q_buf.shape[1]), f32)
    for m in range(mp):
        raw = raw + dot_nt(vec_half[:, m * width : (m + 1) * width], q_buf[m])
    pass_scale = lax.rsqrt(jnp.sum(vec * vec, axis=1, keepdims=True) + unit_epsilon)
    weights = all_live * jnp.exp(score_scale * raw * query_scale * pass_scale)
    doc_index = lax.broadcasted_iota(jnp.int32, weights.shape, 0) // most
    hit = (doc_index == positive[...]).astype(f32)
    mass = jnp.sum(weights, axis=0, keepdims=True)
    hit_mass = jnp.sum(weights * hit, axis=0, keepdims=True)
    loss_out[...] = jnp.log(mass) - jnp.log(hit_mass)
    coef = loss_seed * score_scale * query_scale * (weights / mass - hit * weights / hit_mass)
    norm_term = jnp.sum(coef * raw, axis=1, keepdims=True)
    coef_half = coef.astype(bf16)
    for m in range(mp):
        part = dot_nn(coef_half, q_buf[m])
        for d in range(dp):
            term_send[d, :, m * width : (m + 1) * width] = part[d * passes : (d + 1) * passes].astype(bf16)
    wide = jnp.broadcast_to(norm_term, (pass_total, lane))
    for d in range(dp):
        term_send[d, :, model:] = wide[d * passes : (d + 1) * passes].astype(bf16)

    def term_copy(k):
        to = (dme + k) % dp
        return remote(
            term_send.at[to], term_recv.at[dme], tm_s.at[k - 1], tm_r.at[k - 1], to, me
        )

    for k in range(1, dp):
        term_copy(k).start()
    term_recv[dme] = term_send[dme]
    for k in range(1, dp):
        term_copy(k).wait_recv()
    terms = term_recv[0].astype(f32)
    for d in range(1, dp):
        terms = terms + term_recv[d].astype(f32)
    own_vec = everyone[dme].astype(f32)[:, 0:model]
    own_scale = lax.rsqrt(jnp.sum(own_vec * own_vec, axis=1, keepdims=True) + unit_epsilon)
    change = own_scale * terms[:, 0:model] - own_vec * (
        own_scale * own_scale * own_scale * terms[:, model : model + 1]
    )
    token = (change / divisor).astype(bf16).astype(f32)
    tok_grad[...] = token
    token_half = jnp.concatenate([token, jnp.zeros_like(token)], axis=0).astype(bf16)
    for t in range(hid // tile):
        cols = slice(t * tile, (t + 1) * tile)
        g_row[:, cols] = dot_nt(token_half, wd[cols, :])

    def near_part(j, c):
        return remote(
            near_send.at[c, j], near_recv.at[c, j], ns_s.at[c, j], ns_r.at[c, j], dme, partner
        )

    def far_part(j, c):
        return remote(
            far_send.at[c, j - 1], far_recv.at[c, j - 1], fs_s.at[c, j - 1], fs_r.at[c, j - 1], dme, same(j)
        )

    def backward(c, carry):
        at = chunk_rows(c)
        for i in range(chunk_pass):
            row = g_row[pl.ds(c * chunk_pass + i, 1), :]
            spread = jnp.broadcast_to(row, (L, hid)).astype(bf16)
            here = pl.ds(pl.multiple_of(c * crow + i * L, L), L)
            dgate[i * L : (i + 1) * L, :] = a_buf[here, :] * spread
            dup[i * L : (i + 1) * L, :] = b_buf[here, :] * spread

        def partial(block):
            at_rows = pl.ds(pl.multiple_of(block * width, width), width)
            return dot_nt(dgate[...], wg[at_rows, :]) + dot_nt(dup[...], wu[at_rows, :])

        for j in range(1, far):
            near_send[c, j] = partial(other(j)).astype(bf16)
            near_part(j, c).start()
        for j in range(1, far):
            mine = partial(same(j))
            near_part(j, c).wait_recv()
            far_send[c, j - 1] = (mine + near_recv[c, j].astype(f32)).astype(bf16)
            far_part(j, c).start()
        near_send[c, 0] = partial(other(0)).astype(bf16)
        near_part(0, c).start()
        kept[c] = partial(me)
        return carry

    lax.fori_loop(0, chunks, backward, 0)

    g_half = g_row[...].astype(bf16)
    diagonal = jnp.zeros((2 * passes, L), f32)
    for c in range(chunks):
        found = dot_nt(g_half, c_buf[c * crow : (c + 1) * crow, :])
        for i in range(chunk_pass):
            diagonal = diagonal + jnp.where(
                pool_index == c * chunk_pass + i, found[:, i * L : (i + 1) * L], 0.0
            )
    inner_x[me] = diagonal[0:passes]

    def inner_copy(k):
        return remote(
            inner_x.at[me], inner_x.at[me], in_s.at[k - 1], in_r.at[k - 1], dme, (me + k) % mp
        )

    for k in range(1, mp):
        inner_copy(k).start()
    for k in range(1, mp):
        inner_copy(k).wait_recv()
    inner = inner_x[0]
    for m in range(1, mp):
        inner = inner + inner_x[m]
    inner_col = jnp.transpose(inner / model)
    mask_col = jnp.transpose(mask_row[...])
    own = pl.ds(pl.multiple_of(me * width, width), width)
    own_gain = gain[:, own]
    for c in range(chunks):
        near_part(0, c).wait_recv()
        for j in range(1, far):
            far_part(j, c).wait_recv()
        for i in range(chunk_pass):
            p = c * chunk_pass + i
            piece_rows = slice(i * L, (i + 1) * L)
            summed = kept[c, piece_rows, :] + near_recv[c, 0, piece_rows, :].astype(f32)
            for j in range(1, far):
                summed = summed + far_recv[c, j - 1, piece_rows, :].astype(f32)
            scale = rms[p * L : (p + 1) * L, :]
            own_x = x_buf[me, p * L : (p + 1) * L, :].astype(f32)
            value = (
                tok_grad[p : p + 1, own]
                + scale * own_gain * summed
                - own_x * (scale * scale * inner_col[:, p : p + 1])
            )
            staged[c, piece_rows, :] = jnp.where(mask_col[:, p : p + 1] > 0.0, value, 0.0).astype(bf16)
        pltpu.make_async_copy(staged.at[c], grad_out.at[chunk_rows(c)], out_sem.at[c]).start()

    for c in range(chunks):
        pltpu.make_async_copy(staged.at[c], grad_out.at[chunk_rows(c)], out_sem.at[c]).wait()
    for c in range(chunks + 1):
        near_copy(c).wait_send()
        for j in range(1, far):
            far_copy(j, c).wait_send()
            relay_copy(j, c).wait_send()
    for k in range(1, mp):
        branch_copy(k).wait_send()
        inner_copy(k).wait_send()
    for k in range(1, dp):
        every_copy(k).wait_send()
        term_copy(k).wait_send()
    for c in range(chunks):
        near_part(0, c).wait_send()
        for j in range(1, far):
            near_part(j, c).wait_send()
            far_part(j, c).wait_send()


def per_device(
    hidden_in, token_ids, passage_counts, positive_doc, queries, norm_gain, w_gate, w_up, w_down
):
    dp = lax.axis_size("dp")
    mp = lax.axis_size("mp")
    rows, width = hidden_in.shape
    model, hid = w_gate.shape
    query_rows = queries.shape[0]
    passes = rows // L
    most = passes // passage_counts.shape[0]
    chunks = passes // chunk_pass
    crow = chunk_pass * L
    far = mp // 2
    dims = (dp, mp, far, rows, width, model, hid, passes, most, chunks, crow)
    hbm = pl.BlockSpec(memory_space=pl.ANY)
    vmem = pl.BlockSpec(memory_space=pltpu.VMEM)
    dma = pltpu.SemaphoreType.DMA
    wide = model + lane
    few = max(far - 1, 1)
    loss, grad = pl.pallas_call(
        functools.partial(kernel, dims),
        out_shape=(
            jax.ShapeDtypeStruct((1, query_rows), f32),
            jax.ShapeDtypeStruct((rows, width), bf16),
        ),
        in_specs=[hbm] * 5 + [vmem, pl.BlockSpec(memory_space=pltpu.SMEM), vmem, vmem],
        out_specs=(vmem, hbm),
        scratch_shapes=[
            pltpu.VMEM((mp, rows, width), bf16),
            pltpu.VMEM((mp, query_rows, width), bf16),
            pltpu.VMEM((model, hid), bf16),
            pltpu.VMEM((model, hid), bf16),
            pltpu.VMEM((hid, model), bf16),
            pltpu.VMEM((rows, hid), bf16),
            pltpu.VMEM((rows, hid), bf16),
            pltpu.VMEM((rows, hid), bf16),
            pltpu.VMEM((crow, model), bf16),
            pltpu.VMEM((8, lane), bf16),
            pltpu.VMEM((crow, hid), bf16),
            pltpu.VMEM((crow, hid), bf16),
            pltpu.VMEM((rows, 1), f32),
            pltpu.VMEM((2 * passes, hid), f32),
            pltpu.VMEM((2 * passes, model), f32),
            pltpu.VMEM((mp, passes, model), bf16),
            pltpu.VMEM((dp, passes, wide), bf16),
            pltpu.VMEM((dp, passes, wide), bf16),
            pltpu.VMEM((dp, passes, wide), bf16),
            pltpu.VMEM((passes, model), f32),
            pltpu.VMEM((2 * passes, hid), f32),
            pltpu.VMEM((mp, passes, L), f32),
            pltpu.VMEM((passes, L), f32),
            pltpu.VMEM((chunks, far, crow, width), bf16),
            pltpu.VMEM((chunks, far, crow, width), bf16),
            pltpu.VMEM((chunks, few, crow, width), bf16),
            pltpu.VMEM((chunks, few, crow, width), bf16),
            pltpu.VMEM((chunks, crow, width), f32),
            pltpu.VMEM((chunks, crow, width), bf16),
            dma((5,)),
            dma((chunks,)),
            dma((chunks + 1,)),
            dma((chunks + 1,)),
            dma((few, chunks + 1)),
            dma((few, chunks + 1)),
            dma((few, chunks + 1)),
            dma((few, chunks + 1)),
            dma((mp - 1,)),
            dma((mp - 1,)),
            dma((mp - 1,)),
            dma((mp - 1,)),
            dma((dp - 1,)),
            dma((dp - 1,)),
            dma((dp - 1,)),
            dma((dp - 1,)),
            dma((chunks, far)),
            dma((chunks, far)),
            dma((chunks, few)),
            dma((chunks, few)),
        ],
        compiler_params=pltpu.CompilerParams(
            collective_id=0, has_side_effects=True, vmem_limit_bytes=67000000
        ),
        name="gradcache_step",
    )(
        hidden_in,
        queries,
        w_gate,
        w_up,
        w_down,
        token_ids.reshape(passes, L),
        passage_counts,
        positive_doc.reshape(1, query_rows),
        norm_gain.reshape(1, model),
    )
    return loss.reshape(query_rows), grad


def solution(mesh):
    return jax.shard_map(
        per_device,
        mesh=mesh,
        in_specs=(
            P("dp", "mp"),
            P("dp"),
            P("dp"),
            P("dp"),
            P("dp", "mp"),
            P(),
            P(None, "mp"),
            P(None, "mp"),
            P("mp", None),
        ),
        out_specs=(P("dp"), P("dp", "mp")),
        check_vma=False,
    )
```

profile of v0, /device:TPU:0, one launch (start us, length us, event | category | flops | bytes accessed | tf_op | source)
XLA Modules:
  0.0 95.8 jit_solution(9135763250987885397)
XLA Ops:
  0.6 91.7 %gradcache_step.1 = (f32[1,128]{1,0:T(1,128)}, bf16[1024,512]{1,0:T(8,128)(2,1)}) custom-call(bf16[1024,512]{1,0:T(8,128)(2,1)} %hidden.1, bf16[128,512]{1,0:T(8,128)(2,1)} %queries.1, bf16[2048,1792]{1,0:T(8,128)(2,1)} %w_gate.1, bf16[2048,1792]{1,0:T(8,128)(2,1)} %w_up.1, bf16[1792,2048]{1,0:T(8,128)(2,1)} %w_down.1, s32[8,128]{1,0:T(8,128)} %bitcast.5, ...), custom_call_target="tpu_custom_call" | custom-call | tf_op jit(solution)/shard_map/gradcache_step/pallas_call | solution.py:406
  92.4 1.1 %copy.13 = f32[128]{0:T(128)} copy(f32[128]{0:T(128)} %bitcast.7) | data formatting | bytes 1024
  93.5 2.3 %copy.14 = bf16[1024,512]{1,0:T(8,128)(2,1)} copy(bf16[1024,512]{1,0:T(8,128)(2,1)} %get-tuple-element.9) | data formatting | bytes 2097152
where the time goes:
time: 96 us; the launch traced here: 95.8 us
  Pallas kernels  91.7 us (96%)
  local copies, waits for them, and re-layouts  3.38 us (4%)
    pallas_call x1, Pallas kernels, per_device(): pl.pallas_call(functools.partial(kernel, dims), out_shape=(jax.ShapeDtype...  91.7 us
    unnamed x2, local copies, waits for them, and re-layouts  3.38 us

commit v1 on v0

v1 whole, which is shorter than its diff:
```python
import functools

import jax
import jax.numpy as jnp
from jax import lax
from jax.experimental import pallas as pl
from jax.experimental.pallas import tpu as pltpu
from jax.sharding import PartitionSpec as P

L = 128

pad_token = 128001
score_scale = 20.0
loss_seed = 4096.0
norm_epsilon = 1e-05
unit_epsilon = 1e-06
lane = 128
chunk_pass = 2
MESH = pl.DeviceIdType.MESH
f32 = jnp.float32
bf16 = jnp.bfloat16


def dot_nn(left, right):
    return lax.dot_general(left, right, (((1,), (0,)), ((), ())), preferred_element_type=f32)


def dot_nt(left, right):
    return lax.dot_general(left, right, (((1,), (1,)), ((), ())), preferred_element_type=f32)


def tile_of(width):
    return 256 if width % 256 == 0 else lane


def kernel(
    dims,
    hidden, queries, w_gate, w_up, w_down, tokens, counts, positive, gain,
    loss_out, grad_out,
    x_buf, q_all, pos_all, wg, wu, wd, a_buf, b_buf, c_buf, normed, dgate, dup, rms,
    act_pool, row_pool, branch_send, branch, square_x, raw_x, mass_x, mass_all, tok_x, tok_grad,
    g_row, inner_x,
    mask_row, near_send, near_recv, far_send, far_recv, kept, staged, sum_gate, sum_up,
    load_sem, out_sem, xn_s, xn_r, xf_s, xf_r, xr_s, xr_r, br_s, br_r, in_s, in_r,
    qu_s, qu_r, po_s, po_r, sq_s, sq_r, ra_s, ra_r, ma_s, ma_r, tk_s, tk_r,
    ns_s, ns_r, fs_s, fs_r,
):
    dp, mp, far, rows, width, model, hid, passes, most, chunks, crow, asked = dims
    asked_all = dp * asked
    me = lax.axis_index("mp")
    dme = lax.axis_index("dp")
    chip, core = me // 2, me % 2
    partner = chip * 2 + (1 - core)

    def same(j):
        return ((chip + j + far) % far) * 2 + core

    def other(j):
        return ((chip + j + far) % far) * 2 + (1 - core)

    def chunk_rows(c):
        return pl.ds(pl.multiple_of(c * crow, crow), crow)

    def remote(src, dst, send, recv, d, m):
        return pltpu.make_async_remote_copy(
            src_ref=src, dst_ref=dst, send_sem=send, recv_sem=recv,
            device_id=(d, m), device_id_type=MESH,
        )

    load_x = pltpu.make_async_copy(hidden, x_buf.at[me], load_sem.at[0])
    load_g = pltpu.make_async_copy(w_gate, wg, load_sem.at[1])
    load_u = pltpu.make_async_copy(w_up, wu, load_sem.at[2])
    load_d = pltpu.make_async_copy(w_down, wd, load_sem.at[3])
    load_q = pltpu.make_async_copy(queries, q_all.at[dme], load_sem.at[4])

    barrier = pltpu.get_barrier_semaphore()
    for k in range(1, mp):
        pl.semaphore_signal(barrier, inc=1, device_id=(dme, (me + k) % mp), device_id_type=MESH)
    for k in range(1, dp):
        pl.semaphore_signal(barrier, inc=1, device_id=((dme + k) % dp, me), device_id_type=MESH)
    load_x.start()
    load_g.start()
    load_u.start()
    load_q.start()
    load_d.start()
    pl.semaphore_wait(barrier, mp - 1 + dp - 1)

    def far_copy(j, c):
        return remote(
            hidden.at[chunk_rows(c)], x_buf.at[me, chunk_rows(c)],
            xf_s.at[j - 1, c], xf_r.at[j - 1, c], dme, same(j),
        )

    def near_copy(c):
        return remote(
            hidden.at[chunk_rows(c)], x_buf.at[me, chunk_rows(c)], xn_s.at[c], xn_r.at[c], dme, partner
        )

    def relay_copy(j, c):
        passed = x_buf.at[same(-j), chunk_rows(c)]
        return remote(passed, passed, xr_s.at[j - 1, c], xr_r.at[j - 1, c], dme, partner)

    def relay(c):
        for j in range(1, far):
            far_copy(j, c).wait_recv()
            relay_copy(j, c).start()

    def query_copy(k):
        return remote(
            queries, q_all.at[dme], qu_s.at[k - 1], qu_r.at[k - 1], (dme + k) % dp, me
        )

    def positive_copy(k):
        return remote(
            positive, pos_all.at[dme], po_s.at[k - 1], po_r.at[k - 1], (dme + k) % dp, me
        )

    for c in range(chunks):
        for j in range(1, far):
            far_copy(j, c).start()
        near_copy(c).start()
    for k in range(1, dp):
        query_copy(k).start()
        positive_copy(k).start()
    pos_all[dme] = positive[...]

    pass_index = lax.broadcasted_iota(jnp.int32, (passes, L), 0)
    count = jnp.zeros((passes, L), jnp.int32)
    for d in range(passes // most):
        count = jnp.where(pass_index // most == d, counts[d], count)
    live = (pass_index % most < count).astype(f32)
    mask = jnp.where(tokens[...] != pad_token, live, 0.0)
    mask_row[...] = mask
    divisor = jnp.maximum(jnp.sum(mask, axis=1, keepdims=True), 1.0)
    act_pool[...] = jnp.zeros_like(act_pool)
    row_pool[...] = jnp.zeros_like(row_pool)
    pool_index = lax.broadcasted_iota(jnp.int32, (2 * passes, L), 0)

    tile = tile_of(hid)
    tiles = hid // tile
    last = chunks - 1
    pair = 2 * width

    def select_of(c):
        return jnp.concatenate(
            [
                jnp.where(pool_index == c * chunk_pass + i, mask_row[pl.ds(c * chunk_pass + i, 1), :], 0.0)
                for i in range(chunk_pass)
            ],
            axis=1,
        ).astype(bf16)

    def scale_of(at):
        squares = jnp.zeros((crow, 1), f32)
        for m in range(mp):
            piece_x = x_buf[m, at, :].astype(f32)
            squares = squares + jnp.sum(piece_x * piece_x, axis=1, keepdims=True)
        scale = lax.rsqrt(squares / model + norm_epsilon)
        rms[at, :] = scale
        return scale

    def activate(gate, up, at, cols, select):
        sig = jax.nn.sigmoid(gate)
        b = gate * sig
        a = up * sig * (1.0 + gate * (1.0 - sig))
        hidden_act = (b * up).astype(bf16)
        a_buf[at, cols] = a.astype(bf16)
        b_buf[at, cols] = b.astype(bf16)
        c_buf[at, cols] = (a * gate + b * up).astype(bf16)
        act_pool[:, cols] += dot_nn(select, hidden_act)

    last_rows = slice(last * crow, chunks * crow)

    def gained(m):
        block_gain = gain[:, pl.ds(pl.multiple_of(m * width, width), width)]
        return (x_buf[m, last_rows, :].astype(f32) * block_gain).astype(bf16)

    def block_rows(m, count=1):
        return pl.ds(pl.multiple_of(m * width, width), count * width)

    load_x.wait()
    near_copy(last).wait_recv()
    for i in range(2):
        normed[:, i * width : (i + 1) * width] = gained(chip * 2 + i)
    load_g.wait()
    load_u.wait()
    for t in range(tiles):
        cols = slice(t * tile, (t + 1) * tile)
        if t == tiles // 2:
            relay(0)
        lead = normed[:, 0:pair]
        sum_gate[:, cols] = dot_nn(lead, wg[block_rows(chip * 2, 2), cols])
        sum_up[:, cols] = dot_nn(lead, wu[block_rows(chip * 2, 2), cols])

    def forward(c, carry):
        at = chunk_rows(c)
        near_copy(c).wait_recv()
        for j in range(1, far):
            relay_copy(j, c).wait_recv()
        select = select_of(c)
        scale = scale_of(at)
        for m in range(mp):
            cols = slice(m * width, (m + 1) * width)
            raw_x = x_buf[m, at, :]
            normed[:, cols] = (raw_x.astype(f32) * scale * gain[:, cols]).astype(bf16)
            row_pool[:, cols] += dot_nn(select, raw_x)
        for t in range(tiles):
            cols = slice(t * tile, (t + 1) * tile)
            gate = dot_nn(normed[...], wg[:, cols])
            up = dot_nn(normed[...], wu[:, cols])
            activate(gate, up, at, cols, select)
            if t == max(tiles - 2, 0):
                @pl.when(c + 1 < last)
                def _():
                    relay(c + 1)
        return carry

    lax.fori_loop(0, last, forward, 0)
    relay(last)
    for j in range(1, far):
        normed[:, (j - 1) * width : j * width] = gained(same(-j))
    for t in range(tiles):
        cols = slice(t * tile, (t + 1) * tile)
        for j in range(1, far):
            lead = normed[:, (j - 1) * width : j * width]
            sum_gate[:, cols] += dot_nn(lead, wg[block_rows(same(-j)), cols])
            sum_up[:, cols] += dot_nn(lead, wu[block_rows(same(-j)), cols])
    for j in range(1, far):
        relay_copy(j, last).wait_recv()
    for j in range(1, far):
        normed[:, (j - 1) * width : j * width] = gained(other(-j))
    last_scale = scale_of(last_rows)
    select = select_of(last)
    for t in range(tiles):
        cols = slice(t * tile, (t + 1) * tile)
        gate = sum_gate[:, cols]
        up = sum_up[:, cols]
        for j in range(1, far):
            lead = normed[:, (j - 1) * width : j * width]
            gate = gate + dot_nn(lead, wg[block_rows(other(-j)), cols])
            up = up + dot_nn(lead, wu[block_rows(other(-j)), cols])
        activate(gate * last_scale, up * last_scale, last_rows, cols, select)
    for m in range(mp):
        cols = slice(m * width, (m + 1) * width)
        row_pool[:, cols] += dot_nn(select, x_buf[m, last_rows, :])

    load_d.wait()
    pooled = act_pool[0:passes, :]
    high = pooled.astype(bf16).astype(f32)
    both = jnp.concatenate([high, pooled - high], axis=0).astype(bf16)
    def to_peer(ref, dst, send, recv, k):
        return remote(ref, dst, send.at[k - 1], recv.at[k - 1], dme, (me + k) % mp)

    def block_lanes(m):
        return pl.ds(pl.multiple_of(m * width, width), width)

    def branch_copy(k):
        return to_peer(branch_send.at[k], branch.at[me], br_s, br_r, k)

    for k in range(1, mp):
        part = dot_nn(both, wd[:, block_lanes((me + k) % mp)])
        branch_send[k] = (part[0:passes] + part[passes:]).astype(bf16)
        branch_copy(k).start()
    part = dot_nn(both, wd[:, block_lanes(me)])
    branch[me] = (part[0:passes] + part[passes:]).astype(bf16)

    load_q.wait()
    for k in range(1, dp):
        query_copy(k).wait_recv()
    ones = jnp.ones((2 * passes, width), bf16)
    for d in range(dp):
        query = q_all[d].astype(f32)
        square = query * query
        top = square.astype(bf16)
        rest = (square - top.astype(f32)).astype(bf16)
        square_x[me, :, d * asked : (d + 1) * asked] = (dot_nt(ones, top) + dot_nt(ones, rest))[0:1, :]

    def square_copy(k):
        return to_peer(square_x.at[me], square_x.at[me], sq_s, sq_r, k)

    for k in range(1, mp):
        square_copy(k).start()

    for k in range(1, mp):
        branch_copy(k).wait_recv()
    own = block_lanes(me)
    total = row_pool[0:passes, own]
    for m in range(mp):
        total = total + branch[m].astype(f32)
    vec = (total / divisor).astype(bf16).astype(f32)
    vec_half = jnp.concatenate([vec, jnp.zeros_like(vec)], axis=0).astype(bf16)
    for d in range(dp):
        raw_x[me, :, d * asked : (d + 1) * asked] = dot_nt(vec_half, q_all[d])[0:passes]
    raw_x[me, :, asked_all:] = jnp.broadcast_to(
        jnp.sum(vec * vec, axis=1, keepdims=True), (passes, lane)
    )

    def raw_copy(k):
        return to_peer(raw_x.at[me], raw_x.at[me], ra_s, ra_r, k)

    for k in range(1, mp):
        raw_copy(k).start()
    for k in range(1, dp):
        positive_copy(k).wait_recv()
    asked_for = jnp.concatenate([pos_all[d] for d in range(dp)], axis=1)
    doc_index = dme * (passes // most) + lax.broadcasted_iota(jnp.int32, (passes, asked_all), 0) // most
    hit = (doc_index == asked_for).astype(f32)
    for k in range(1, mp):
        square_copy(k).wait_recv()
    query_square = square_x[0]
    for m in range(1, mp):
        query_square = query_square + square_x[m]
    query_scale = lax.rsqrt(query_square + unit_epsilon)
    for k in range(1, mp):
        raw_copy(k).wait_recv()

    summed = raw_x[0]
    for m in range(1, mp):
        summed = summed + raw_x[m]
    raw = summed[:, 0:asked_all]
    pass_scale = lax.rsqrt(summed[:, asked_all : asked_all + 1] + unit_epsilon)
    weights = live[:, 0:1] * jnp.exp(score_scale * raw * query_scale * pass_scale)
    mass_x[dme] = jnp.concatenate(
        [jnp.sum(weights, axis=0, keepdims=True), jnp.sum(weights * hit, axis=0, keepdims=True)], axis=0
    )

    def mass_copy(k):
        return remote(
            mass_x.at[dme], mass_x.at[dme], ma_s.at[k - 1], ma_r.at[k - 1], (dme + k) % dp, me
        )

    for k in range(1, dp):
        mass_copy(k).start()
    for k in range(1, dp):
        mass_copy(k).wait_recv()
    masses = mass_x[0]
    for d in range(1, dp):
        masses = masses + mass_x[d]
    mass_all[...] = masses
    mass = masses[0:1, :]
    hit_mass = masses[1:2, :]
    coef = loss_seed * score_scale * query_scale * (weights / mass - hit * weights / hit_mass)
    norm_term = jnp.sum(coef * raw, axis=1, keepdims=True)
    coef_half = jnp.concatenate([coef, jnp.zeros_like(coef)], axis=0).astype(bf16)
    weighted = jnp.zeros((2 * passes, width), f32)
    for d in range(dp):
        weighted = weighted + dot_nn(coef_half[:, d * asked : (d + 1) * asked], q_all[d])
    change = pass_scale * weighted[0:passes] - vec * (
        pass_scale * pass_scale * pass_scale * norm_term
    )
    token = (change / divisor).astype(bf16)
    tok_grad[...] = token.astype(f32)
    tok_x[me] = token

    def token_copy(k):
        return to_peer(tok_x.at[me], tok_x.at[me], tk_s, tk_r, k)

    for k in range(1, mp):
        token_copy(k).start()
    own_asked = pl.ds(pl.multiple_of(dme * asked, asked), asked)
    loss_out[...] = jnp.log(mass_all[0:1, own_asked]) - jnp.log(mass_all[1:2, own_asked])
    for k in range(1, mp):
        token_copy(k).wait_recv()
    token = jnp.concatenate([tok_x[m].astype(f32) for m in range(mp)], axis=1)
    token_half = jnp.concatenate([token, jnp.zeros_like(token)], axis=0).astype(bf16)
    for t in range(hid // tile):
        cols = slice(t * tile, (t + 1) * tile)
        g_row[:, cols] = dot_nt(token_half, wd[cols, :])

    def near_part(j, c):
        return remote(
            near_send.at[c, j], near_recv.at[c, j], ns_s.at[c, j], ns_r.at[c, j], dme, partner
        )

    def far_part(j, c):
        return remote(
            far_send.at[c, j - 1], far_recv.at[c, j - 1], fs_s.at[c, j - 1], fs_r.at[c, j - 1], dme, same(j)
        )

    def backward(c, carry):
        at = chunk_rows(c)
        for i in range(chunk_pass):
            row = g_row[pl.ds(c * chunk_pass + i, 1), :]
            spread = jnp.broadcast_to(row, (L, hid)).astype(bf16)
            here = pl.ds(pl.multiple_of(c * crow + i * L, L), L)
            dgate[i * L : (i + 1) * L, :] = a_buf[here, :] * spread
            dup[i * L : (i + 1) * L, :] = b_buf[here, :] * spread

        def partial(block):
            at_rows = pl.ds(pl.multiple_of(block * width, width), width)
            return dot_nt(dgate[...], wg[at_rows, :]) + dot_nt(dup[...], wu[at_rows, :])

        for j in range(1, far):
            near_send[c, j] = partial(other(j)).astype(bf16)
            near_part(j, c).start()
        for j in range(1, far):
            mine = partial(same(j))
            near_part(j, c).wait_recv()
            far_send[c, j - 1] = (mine + near_recv[c, j].astype(f32)).astype(bf16)
            far_part(j, c).start()
        near_send[c, 0] = partial(other(0)).astype(bf16)
        near_part(0, c).start()
        kept[c] = partial(me)
        return carry

    backward(0, 0)

    g_half = g_row[...].astype(bf16)
    diagonal = jnp.zeros((2 * passes, L), f32)
    for c in range(chunks):
        found = dot_nt(g_half, c_buf[c * crow : (c + 1) * crow, :])
        for i in range(chunk_pass):
            diagonal = diagonal + jnp.where(
                pool_index == c * chunk_pass + i, found[:, i * L : (i + 1) * L], 0.0
            )
    inner_x[me] = diagonal[0:passes]

    def inner_copy(k):
        return remote(
            inner_x.at[me], inner_x.at[me], in_s.at[k - 1], in_r.at[k - 1], dme, (me + k) % mp
        )

    for k in range(1, mp):
        inner_copy(k).start()
    lax.fori_loop(1, chunks, backward, 0)

    for k in range(1, mp):
        inner_copy(k).wait_recv()
    inner = inner_x[0]
    for m in range(1, mp):
        inner = inner + inner_x[m]
    inner_col = jnp.transpose(inner / model)
    mask_col = jnp.transpose(mask_row[...])
    own_gain = gain[:, own]
    for c in range(chunks):
        near_part(0, c).wait_recv()
        for j in range(1, far):
            far_part(j, c).wait_recv()
        for i in range(chunk_pass):
            p = c * chunk_pass + i
            piece_rows = slice(i * L, (i + 1) * L)
            summed = kept[c, piece_rows, :] + near_recv[c, 0, piece_rows, :].astype(f32)
            for j in range(1, far):
                summed = summed + far_recv[c, j - 1, piece_rows, :].astype(f32)
            scale = rms[p * L : (p + 1) * L, :]
            own_x = x_buf[me, p * L : (p + 1) * L, :].astype(f32)
            value = (
                tok_grad[p : p + 1, :]
                + scale * own_gain * summed
                - own_x * (scale * scale * inner_col[:, p : p + 1])
            )
            staged[c, piece_rows, :] = jnp.where(mask_col[:, p : p + 1] > 0.0, value, 0.0).astype(bf16)
        pltpu.make_async_copy(staged.at[c], grad_out.at[chunk_rows(c)], out_sem.at[c]).start()

    for c in range(chunks):
        pltpu.make_async_copy(staged.at[c], grad_out.at[chunk_rows(c)], out_sem.at[c]).wait()
    for c in range(chunks):
        near_copy(c).wait_send()
        for j in range(1, far):
            far_copy(j, c).wait_send()
            relay_copy(j, c).wait_send()
    for k in range(1, mp):
        branch_copy(k).wait_send()
        square_copy(k).wait_send()
        raw_copy(k).wait_send()
        token_copy(k).wait_send()
        inner_copy(k).wait_send()
    for k in range(1, dp):
        query_copy(k).wait_send()
        positive_copy(k).wait_send()
        mass_copy(k).wait_send()
    for c in range(chunks):
        near_part(0, c).wait_send()
        for j in range(1, far):
            near_part(j, c).wait_send()
            far_part(j, c).wait_send()


def per_device(
    hidden_in, token_ids, passage_counts, positive_doc, queries, norm_gain, w_gate, w_up, w_down
):
    dp = lax.axis_size("dp")
    mp = lax.axis_size("mp")
    rows, width = hidden_in.shape
    model, hid = w_gate.shape
    query_rows = queries.shape[0]
    passes = rows // L
    most = passes // passage_counts.shape[0]
    chunks = passes // chunk_pass
    crow = chunk_pass * L
    far = mp // 2
    dims = (dp, mp, far, rows, width, model, hid, passes, most, chunks, crow, query_rows)
    hbm = pl.BlockSpec(memory_space=pl.ANY)
    vmem = pl.BlockSpec(memory_space=pltpu.VMEM)
    dma = pltpu.SemaphoreType.DMA
    few = max(far - 1, 1)
    loss, grad = pl.pallas_call(
        functools.partial(kernel, dims),
        out_shape=(
            jax.ShapeDtypeStruct((1, query_rows), f32),
            jax.ShapeDtypeStruct((rows, width), bf16),
        ),
        in_specs=[hbm] * 5 + [vmem, pl.BlockSpec(memory_space=pltpu.SMEM), vmem, vmem],
        out_specs=(vmem, hbm),
        scratch_shapes=[
            pltpu.VMEM((mp, rows, width), bf16),
            pltpu.VMEM((dp, query_rows, width), bf16),
            pltpu.VMEM((dp, 1, query_rows), jnp.int32),
            pltpu.VMEM((model, hid), bf16),
            pltpu.VMEM((model, hid), bf16),
            pltpu.VMEM((hid, model), bf16),
            pltpu.VMEM((rows, hid), bf16),
            pltpu.VMEM((rows, hid), bf16),
            pltpu.VMEM((rows, hid), bf16),
            pltpu.VMEM((crow, model), bf16),
            pltpu.VMEM((crow, hid), bf16),
            pltpu.VMEM((crow, hid), bf16),
            pltpu.VMEM((rows, 1), f32),
            pltpu.VMEM((2 * passes, hid), f32),
            pltpu.VMEM((2 * passes, model), f32),
            pltpu.VMEM((mp, passes, width), bf16),
            pltpu.VMEM((mp, passes, width), bf16),
            pltpu.VMEM((mp, 1, dp * query_rows), f32),
            pltpu.VMEM((mp, passes, dp * query_rows + lane), f32),
            pltpu.VMEM((dp, 2, dp * query_rows), f32),
            pltpu.VMEM((2, dp * query_rows), f32),
            pltpu.VMEM((mp, passes, width), bf16),
            pltpu.VMEM((passes, width), f32),
            pltpu.VMEM((2 * passes, hid), f32),
            pltpu.VMEM((mp, passes, L), f32),
            pltpu.VMEM((passes, L), f32),
            pltpu.VMEM((chunks, far, crow, width), bf16),
            pltpu.VMEM((chunks, far, crow, width), bf16),
            pltpu.VMEM((chunks, few, crow, width), bf16),
            pltpu.VMEM((chunks, few, crow, width), bf16),
            pltpu.VMEM((chunks, crow, width), f32),
            pltpu.VMEM((chunks, crow, width), bf16),
            pltpu.VMEM((crow, hid), f32),
            pltpu.VMEM((crow, hid), f32),
            dma((5,)),
            dma((chunks,)),
            dma((chunks,)),
            dma((chunks,)),
            dma((few, chunks)),
            dma((few, chunks)),
            dma((few, chunks)),
            dma((few, chunks)),
            dma((mp - 1,)),
            dma((mp - 1,)),
            dma((mp - 1,)),
            dma((mp - 1,)),
            dma((dp - 1,)),
            dma((dp - 1,)),
            dma((dp - 1,)),
            dma((dp - 1,)),
            dma((mp - 1,)),
            dma((mp - 1,)),
            dma((mp - 1,)),
            dma((mp - 1,)),
            dma((dp - 1,)),
            dma((dp - 1,)),
            dma((mp - 1,)),
            dma((mp - 1,)),
            dma((chunks, far)),
            dma((chunks, far)),
            dma((chunks, few)),
            dma((chunks, few)),
        ],
        compiler_params=pltpu.CompilerParams(
            collective_id=0, has_side_effects=True, vmem_limit_bytes=67000000
        ),
        name="gradcache_step",
    )(
        hidden_in,
        queries,
        w_gate,
        w_up,
        w_down,
        token_ids.reshape(passes, L),
        passage_counts,
        positive_doc.reshape(1, query_rows),
        norm_gain.reshape(1, model),
    )
    def hand_on(loss_in, grad_in, loss_to, grad_to):
        loss_to[...] = loss_in[0, :]
        grad_to[...] = grad_in[...]

    return tuple(
        pl.pallas_call(
            hand_on,
            grid=(2,),
            out_shape=(
                jax.ShapeDtypeStruct((query_rows,), f32),
                jax.ShapeDtypeStruct((rows, width), bf16),
            ),
            in_specs=[
                pl.BlockSpec((1, query_rows), lambda i: (0, 0)),
                pl.BlockSpec((rows // 2, width), lambda i: (i, 0)),
            ],
            out_specs=(
                pl.BlockSpec((query_rows,), lambda i: (0,)),
                pl.BlockSpec((rows // 2, width), lambda i: (i, 0)),
            ),
            name="hand_on",
        )(loss, grad)
    )


def solution(mesh):
    return jax.shard_map(
        per_device,
        mesh=mesh,
        in_specs=(
            P("dp", "mp"),
            P("dp"),
            P("dp"),
            P("dp"),
            P("dp", "mp"),
            P(),
            P(None, "mp"),
            P(None, "mp"),
            P("mp", None),
        ),
        out_specs=(P("dp"), P("dp", "mp")),
        check_vma=False,
    )
```

time: 96 us -> 86.9 us (0.905)
  Pallas kernels: 91.7 us -> 86 us
  local copies, waits for them, and re-layouts: 3.38 us -> 0 us
    pallas_call x1, Pallas kernels: 91.7 us -> 84 us  [per_device(): pl.pallas_call(functools.partial(kernel, dims), out_shape=(jax.ShapeDtype...]
    unnamed x2 -> x0, local copies, waits for them, and re-layouts: 3.38 us -> none
    pallas_call x0 -> x1, Pallas kernels: none -> 2.06 us  [per_device(): pl.pallas_call(hand_on, grid=(2,), out_shape=(jax.ShapeDtypeStruct((query...]
where the time goes in v1:
time: 86.9 us; the launch traced here: 86.7 us
  Pallas kernels  86 us (99%)
    pallas_call x1, Pallas kernels, per_device(): pl.pallas_call(functools.partial(kernel, dims), out_shape=(jax.ShapeDtype...  84 us
    pallas_call x1, Pallas kernels, per_device(): pl.pallas_call(hand_on, grid=(2,), out_shape=(jax.ShapeDtypeStruct((query...  2.06 us

profile of v1, /device:TPU:0, one launch (start us, length us, event | category | flops | bytes accessed | tf_op | source)
XLA Modules:
  0.0 86.7 jit_solution(14931906904598381588)
XLA Ops:
  0.6 84.0 %gradcache_step.1 = (f32[1,128]{1,0:T(1,128)}, bf16[1024,512]{1,0:T(8,128)(2,1)}) custom-call(bf16[1024,512]{1,0:T(8,128)(2,1)} %hidden.1, bf16[128,512]{1,0:T(8,128)(2,1)} %queries.1, bf16[2048,1792]{1,0:T(8,128)(2,1)} %w_gate.1, bf16[2048,1792]{1,0:T(8,128)(2,1)} %w_up.1, bf16[1792,2048]{1,0:T(8,128)(2,1)} %w_down.1, s32[8,128]{1,0:T(8,128)} %bitcast.4, ...), custom_call_target="tpu_custom_call" | custom-call | tf_op jit(solution)/shard_map/gradcache_step/pallas_call | solution.py:497
  84.6 2.1 %hand_on.1 = (f32[128]{0:T(128)}, bf16[1024,512]{1,0:T(8,128)(2,1)}) custom-call(f32[1,128]{1,0:T(1,128)} %get-tuple-element.4.loss_in, bf16[1024,512]{1,0:T(8,128)(2,1)} %get-tuple-element.5.grad_in), custom_call_target="tpu_custom_call" | custom-call | tf_op jit(solution)/shard_map/hand_on/pallas_call | solution.py:589

commit v2 on v1

--- a/solution.py
+++ b/solution.py
@@ -138,7 +138,6 @@
 
     tile = tile_of(hid)
     tiles = hid // tile
-    last = chunks - 1
     pair = 2 * width
 
     def select_of(c):
@@ -169,28 +168,29 @@
         c_buf[at, cols] = (a * gate + b * up).astype(bf16)
         act_pool[:, cols] += dot_nn(select, hidden_act)
 
-    last_rows = slice(last * crow, chunks * crow)
-
-    def gained(m):
+    late = max(chunks - 2, 0)
+
+    def gained(m, c):
         block_gain = gain[:, pl.ds(pl.multiple_of(m * width, width), width)]
-        return (x_buf[m, last_rows, :].astype(f32) * block_gain).astype(bf16)
+        return (x_buf[m, c * crow : (c + 1) * crow, :].astype(f32) * block_gain).astype(bf16)
 
     def block_rows(m, count=1):
         return pl.ds(pl.multiple_of(m * width, width), count * width)
 
     load_x.wait()
-    near_copy(last).wait_recv()
-    for i in range(2):
-        normed[:, i * width : (i + 1) * width] = gained(chip * 2 + i)
     load_g.wait()
     load_u.wait()
-    for t in range(tiles):
-        cols = slice(t * tile, (t + 1) * tile)
-        if t == tiles // 2:
-            relay(0)
-        lead = normed[:, 0:pair]
-        sum_gate[:, cols] = dot_nn(lead, wg[block_rows(chip * 2, 2), cols])
-        sum_up[:, cols] = dot_nn(lead, wu[block_rows(chip * 2, 2), cols])
+    for c in range(chunks - 1, late - 1, -1):
+        near_copy(c).wait_recv()
+        for i in range(2):
+            normed[:, i * width : (i + 1) * width] = gained(chip * 2 + i, c)
+        for t in range(tiles):
+            cols = slice(t * tile, (t + 1) * tile)
+            if c == late and t == tiles // 2:
+                relay(0)
+            lead = normed[:, 0:pair]
+            sum_gate[c - late, :, cols] = dot_nn(lead, wg[block_rows(chip * 2, 2), cols])
+            sum_up[c - late, :, cols] = dot_nn(lead, wu[block_rows(chip * 2, 2), cols])
 
     def forward(c, carry):
         at = chunk_rows(c)
@@ -209,40 +209,43 @@
             gate = dot_nn(normed[...], wg[:, cols])
             up = dot_nn(normed[...], wu[:, cols])
             activate(gate, up, at, cols, select)
-            if t == max(tiles - 2, 0):
-                @pl.when(c + 1 < last)
+            if t == tiles // 2 + 1:
+                @pl.when(c + 1 < late)
                 def _():
                     relay(c + 1)
         return carry
 
-    lax.fori_loop(0, last, forward, 0)
-    relay(last)
-    for j in range(1, far):
-        normed[:, (j - 1) * width : j * width] = gained(same(-j))
-    for t in range(tiles):
-        cols = slice(t * tile, (t + 1) * tile)
-        for j in range(1, far):
-            lead = normed[:, (j - 1) * width : j * width]
-            sum_gate[:, cols] += dot_nn(lead, wg[block_rows(same(-j)), cols])
-            sum_up[:, cols] += dot_nn(lead, wu[block_rows(same(-j)), cols])
-    for j in range(1, far):
-        relay_copy(j, last).wait_recv()
-    for j in range(1, far):
-        normed[:, (j - 1) * width : j * width] = gained(other(-j))
-    last_scale = scale_of(last_rows)
-    select = select_of(last)
-    for t in range(tiles):
-        cols = slice(t * tile, (t + 1) * tile)
-        gate = sum_gate[:, cols]
-        up = sum_up[:, cols]
-        for j in range(1, far):
-            lead = normed[:, (j - 1) * width : j * width]
-            gate = gate + dot_nn(lead, wg[block_rows(other(-j)), cols])
-            up = up + dot_nn(lead, wu[block_rows(other(-j)), cols])
-        activate(gate * last_scale, up * last_scale, last_rows, cols, select)
-    for m in range(mp):
-        cols = slice(m * width, (m + 1) * width)
-        row_pool[:, cols] += dot_nn(select, x_buf[m, last_rows, :])
+    lax.fori_loop(0, late, forward, 0)
+    for c in range(late, chunks):
+        at = slice(c * crow, (c + 1) * crow)
+        if c > 0:
+            relay(c)
+        for j in range(1, far):
+            normed[:, (j - 1) * width : j * width] = gained(same(-j), c)
+        for t in range(tiles):
+            cols = slice(t * tile, (t + 1) * tile)
+            for j in range(1, far):
+                lead = normed[:, (j - 1) * width : j * width]
+                sum_gate[c - late, :, cols] += dot_nn(lead, wg[block_rows(same(-j)), cols])
+                sum_up[c - late, :, cols] += dot_nn(lead, wu[block_rows(same(-j)), cols])
+        for j in range(1, far):
+            relay_copy(j, c).wait_recv()
+        for j in range(1, far):
+            normed[:, (j - 1) * width : j * width] = gained(other(-j), c)
+        late_scale = scale_of(at)
+        select = select_of(c)
+        for t in range(tiles):
+            cols = slice(t * tile, (t + 1) * tile)
+            gate = sum_gate[c - late, :, cols]
+            up = sum_up[c - late, :, cols]
+            for j in range(1, far):
+                lead = normed[:, (j - 1) * width : j * width]
+                gate = gate + dot_nn(lead, wg[block_rows(other(-j)), cols])
+                up = up + dot_nn(lead, wu[block_rows(other(-j)), cols])
+            activate(gate * late_scale, up * late_scale, at, cols, select)
+        for m in range(mp):
+            cols = slice(m * width, (m + 1) * width)
+            row_pool[:, cols] += dot_nn(select, x_buf[m, at, :])
 
     load_d.wait()
     pooled = act_pool[0:passes, :]
@@ -377,6 +380,11 @@
             far_send.at[c, j - 1], far_recv.at[c, j - 1], fs_s.at[c, j - 1], fs_r.at[c, j - 1], dme, same(j)
         )
 
+    def inner_copy(k):
+        return remote(
+            inner_x.at[me], inner_x.at[me], in_s.at[k - 1], in_r.at[k - 1], dme, (me + k) % mp
+        )
+
     def backward(c, carry):
         at = chunk_rows(c)
         for i in range(chunk_pass):
@@ -401,28 +409,24 @@
         near_send[c, 0] = partial(other(0)).astype(bf16)
         near_part(0, c).start()
         kept[c] = partial(me)
+
+        @pl.when(c == 0)
+        def _():
+            g_half = g_row[...].astype(bf16)
+            diagonal = jnp.zeros((2 * passes, L), f32)
+            for c in range(chunks):
+                found = dot_nt(g_half, c_buf[c * crow : (c + 1) * crow, :])
+                for i in range(chunk_pass):
+                    diagonal = diagonal + jnp.where(
+                        pool_index == c * chunk_pass + i, found[:, i * L : (i + 1) * L], 0.0
+                    )
+            inner_x[me] = diagonal[0:passes]
+            for k in range(1, mp):
+                inner_copy(k).start()
+
         return carry
 
-    backward(0, 0)
-
-    g_half = g_row[...].astype(bf16)
-    diagonal = jnp.zeros((2 * passes, L), f32)
-    for c in range(chunks):
-        found = dot_nt(g_half, c_buf[c * crow : (c + 1) * crow, :])
-        for i in range(chunk_pass):
-            diagonal = diagonal + jnp.where(
-                pool_index == c * chunk_pass + i, found[:, i * L : (i + 1) * L], 0.0
-            )
-    inner_x[me] = diagonal[0:passes]
-
-    def inner_copy(k):
-        return remote(
-            inner_x.at[me], inner_x.at[me], in_s.at[k - 1], in_r.at[k - 1], dme, (me + k) % mp
-        )
-
-    for k in range(1, mp):
-        inner_copy(k).start()
-    lax.fori_loop(1, chunks, backward, 0)
+    lax.fori_loop(0, chunks, backward, 0)
 
     for k in range(1, mp):
         inner_copy(k).wait_recv()
@@ -535,8 +539,8 @@
             pltpu.VMEM((chunks, few, crow, width), bf16),
             pltpu.VMEM((chunks, crow, width), f32),
             pltpu.VMEM((chunks, crow, width), bf16),
-            pltpu.VMEM((crow, hid), f32),
-            pltpu.VMEM((crow, hid), f32),
+            pltpu.VMEM((min(chunks, 2), crow, hid), f32),
+            pltpu.VMEM((min(chunks, 2), crow, hid), f32),
             dma((5,)),
             dma((chunks,)),
             dma((chunks,)),

time: 86.9 us -> 84.8 us (0.976)
  Pallas kernels: 86 us -> 83.9 us
    pallas_call x1, Pallas kernels: 84 us -> 81.9 us  [per_device(): pl.pallas_call(functools.partial(kernel, dims), out_shape=(jax.ShapeDtype...]
where the time goes in v2:
time: 84.8 us; the launch traced here: 84.6 us
  Pallas kernels  83.9 us (99%)
    pallas_call x1, Pallas kernels, per_device(): pl.pallas_call(functools.partial(kernel, dims), out_shape=(jax.ShapeDtype...  81.9 us
    pallas_call x1, Pallas kernels, per_device(): pl.pallas_call(hand_on, grid=(2,), out_shape=(jax.ShapeDtypeStruct((query...  2.06 us

profile of v2, /device:TPU:0, one launch (start us, length us, event | category | flops | bytes accessed | tf_op | source)
XLA Modules:
  0.0 84.6 jit_solution(6363193257393960192)
XLA Ops:
  0.6 81.9 %gradcache_step.1 = (f32[1,128]{1,0:T(1,128)}, bf16[1024,512]{1,0:T(8,128)(2,1)}) custom-call(bf16[1024,512]{1,0:T(8,128)(2,1)} %hidden.1, bf16[128,512]{1,0:T(8,128)(2,1)} %queries.1, bf16[2048,1792]{1,0:T(8,128)(2,1)} %w_gate.1, bf16[2048,1792]{1,0:T(8,128)(2,1)} %w_up.1, bf16[1792,2048]{1,0:T(8,128)(2,1)} %w_down.1, s32[8,128]{1,0:T(8,128)} %bitcast.4, ...), custom_call_target="tpu_custom_call" | custom-call | tf_op jit(solution)/shard_map/gradcache_step/pallas_call | solution.py:501
  82.5 2.1 %hand_on.1 = (f32[128]{0:T(128)}, bf16[1024,512]{1,0:T(8,128)(2,1)}) custom-call(f32[1,128]{1,0:T(1,128)} %get-tuple-element.4.loss_in, bf16[1024,512]{1,0:T(8,128)(2,1)} %get-tuple-element.5.grad_in), custom_call_target="tpu_custom_call" | custom-call | tf_op jit(solution)/shard_map/hand_on/pallas_call | solution.py:593
